TPU v7x, 32 devices: a whole 2x2x4 slice. The times are simulated.
32 devices in a mesh: lat: 16 (over z, y, core), ch: 2 (over x).
Axes of the slice: x: 2, y: 2, z: 4, core: 2. Of those that a mesh axis runs over, the one named last changes fastest.
Arguments:
- tokens: bfloat16 [16, 64, 138240], P(None, 'lat', 'ch'), may hold values from -60 to 60
- norm_gain: float32 [768], P('ch'), may hold values from 0.25 to 1.75
- norm_shift: float32 [768], P('ch'), may hold values from -1.5 to 1.5
- first_weight: float32 [2, 8, 96, 96], P(None, 'ch'), may hold values from -0.625 to 0.625
- first_bias: float32 [2, 8, 96], P(None, 'ch'), may hold values from -1.5 to 1.5
- second_weight: float32 [2, 8, 96, 96], P(None, 'ch'), may hold values from -0.625 to 0.625
- second_bias: float32 [2, 8, 96], P(None, 'ch'), may hold values from -1.5 to 1.5
- upstream: bfloat16 [16, 64, 138240], P(None, 'lat', 'ch'), may hold values from -6 to 6
Outputs:
- result: bfloat16 [16, 64, 138240], P(None, 'lat', 'ch')
- grad_tokens: bfloat16 [16, 64, 138240], P(None, 'lat', 'ch')
- grad_first_weight: float32 [2, 8, 96, 96], P(None, 'ch')
- grad_first_bias: float32 [2, 8, 96], P(None, 'ch')
- grad_second_weight: float32 [2, 8, 96, 96], P(None, 'ch')
- grad_second_bias: float32 [2, 8, 96], P(None, 'ch')
- grad_norm_gain: float32 [768], P('ch')
- grad_norm_shift: float32 [768], P('ch')
All inputs are finite; a program needn't handle non-finite values.
Results may differ from a plain program's by a relative error of at most 0.0086.
Values may be sent and summed in bfloat16 or wider, within the bound.
A program may use at most 384 MiB of HBM per device.

v0:
```python
import math

import jax
import jax.numpy as jnp
from jax import lax
from jax.sharding import PartitionSpec as P

EMBED = 768


layer_eps = 1e-05
shrink_level = 0.1
fast = lax.Precision.HIGH


def angle_table(length, columns):
    row_index = lax.broadcasted_iota(jnp.int32, (length, columns), 0)
    col_index = lax.broadcasted_iota(jnp.int32, (length, columns), 1)
    return 2.0 * math.pi / length * (row_index * col_index % length).astype(jnp.float32)


def longitude_tables(length):
    modes_count = length // 2 + 1
    angles = angle_table(length, modes_count)
    factor = 1.0 / math.sqrt(length)
    mode_index = lax.broadcasted_iota(jnp.int32, (1, modes_count), 1)
    doubled = jnp.where((mode_index == 0) | (mode_index * 2 == length), 1.0, 2.0)
    forward_cos = jnp.cos(angles) * factor
    forward_sin = -jnp.sin(angles) * factor
    return (
        forward_cos,
        forward_sin,
        jnp.transpose(forward_cos * doubled),
        jnp.transpose(forward_sin * doubled),
    )


def contract(spec, left, right):
    return jnp.einsum(spec, left, right, precision=fast)


def row_forward(field_in):
    tables = longitude_tables(field_in.shape[3])
    table = jnp.stack((tables[0], tables[1]))
    return contract("bhcw,pwk->pbhkc", field_in, table)


def row_inverse(spectra):
    length = 2 * (spectra.shape[3] - 1)
    tables = longitude_tables(length)
    table = jnp.stack((tables[2], tables[3]))
    return contract("pbhkc,pkw->bhcw", spectra, table)


def latitude_transform(spectra, direction):
    height = spectra.shape[2]
    angles = angle_table(height, height)
    cosine = jnp.cos(angles) / math.sqrt(height)
    sine_part = direction * jnp.sin(angles) / math.sqrt(height)
    table = jnp.stack((jnp.stack((cosine, -sine_part)), jnp.stack((sine_part, cosine))))
    return contract("rpmh,pbhkc->rbmkc", table, spectra)


def complex_matrix(weight):
    return jnp.stack((jnp.stack((weight[0], weight[1])), jnp.stack((-weight[1], weight[0]))))


def block_mix(values, weight):
    return contract("pbhknc,prncd->rbhknd", values, complex_matrix(weight))


def smooth_gelu(values):
    return (
        0.5
        * values
        * (
            1.0
            + jnp.tanh(math.sqrt(2.0 / math.pi) * (values + 0.044715 * values * values * values))
        )
    )


def spectral_mlp(spectra, params):
    first_weight, first_bias, second_weight, second_bias = params
    dims_shape = spectra.shape
    groups = first_weight.shape[1]
    block_width = first_weight.shape[2]
    spectra = spectra.reshape(dims_shape[:-1] + (groups, block_width))
    hidden = smooth_gelu(block_mix(spectra, first_weight) + first_bias[:, None, None, None])
    mixed = block_mix(hidden, second_weight) + second_bias[:, None, None, None]
    mixed = mixed - shrink_level * jnp.tanh(mixed / shrink_level)
    return mixed.reshape(dims_shape)


def column_spectral(spectra, params):
    spectra = latitude_transform(spectra, -1.0)
    return latitude_transform(spectral_mlp(spectra, params), 1.0)


def channel_sums(first_term, second_term):
    return lax.psum((jnp.sum(first_term, axis=-2), jnp.sum(second_term, axis=-2)), "ch")


def spectra_columns(spectra):
    sent = spectra.astype(jnp.bfloat16)
    moved = lax.all_to_all(sent, "lat", split_axis=1, concat_axis=2, tiled=True)
    return moved.astype(jnp.float32)


def spectra_rows(spectra):
    sent = spectra.astype(jnp.bfloat16)
    moved = lax.all_to_all(sent, "lat", split_axis=2, concat_axis=1, tiled=True)
    return moved.astype(jnp.float32)


def body(
    tokens, norm_gain, norm_shift, first_weight, first_bias, second_weight, second_bias, upstream
):
    params = (first_weight, first_bias, second_weight, second_bias)
    samples, rows_here, merged = tokens.shape
    channels = norm_gain.shape[0]
    width = merged // channels
    field_shape = (samples, rows_here, channels, width)
    gain_column = norm_gain[:, None]
    shift_column = norm_shift[:, None]
    as_float = tokens.reshape(field_shape).astype(jnp.float32)
    totals, squares = channel_sums(as_float, as_float * as_float)
    center = totals[..., None, :] / EMBED
    variance = squares[..., None, :] / EMBED - center * center
    inv_scale = lax.rsqrt(variance + layer_eps)
    standard = (as_float - center) * inv_scale
    normed = lax.optimization_barrier((standard * gain_column + shift_column).astype(jnp.bfloat16))
    normed_float = normed.astype(jnp.float32)
    grad_out = upstream.reshape(field_shape).astype(jnp.float32)
    spectra, forward_pull = jax.vjp(row_forward, normed_float)
    columns = spectra_columns(spectra)
    mixed_spec, column_pull = jax.vjp(column_spectral, columns, params)
    returned = spectra_rows(mixed_spec)
    filtered_float, inverse_pull = jax.vjp(row_inverse, returned)
    filtered = lax.optimization_barrier(filtered_float.astype(jnp.bfloat16))
    cot_columns = spectra_columns(inverse_pull(grad_out)[0])
    spectra_grad, param_grads = column_pull(cot_columns)
    row_grad = forward_pull(spectra_rows(spectra_grad))[0]
    spectral_grad = lax.optimization_barrier(row_grad.astype(jnp.bfloat16))
    result = (as_float + normed_float + filtered.astype(jnp.float32)).astype(jnp.bfloat16)
    normed_grad = grad_out + spectral_grad.astype(jnp.float32)
    gain_part = jnp.sum(normed_grad * standard, axis=(0, 1, 3))
    shift_part = jnp.sum(normed_grad, axis=(0, 1, 3))
    standard_grad = normed_grad * gain_column
    grad_mean, grad_cross = channel_sums(standard_grad, standard_grad * standard)
    grad_tokens = (
        grad_out
        + inv_scale
        * (
            standard_grad
            - grad_mean[..., None, :] / EMBED
            - standard * (grad_cross[..., None, :] / EMBED)
        )
    ).astype(jnp.bfloat16)
    summed = lax.psum(
        (param_grads[0], param_grads[1], param_grads[2], param_grads[3], gain_part, shift_part),
        "lat",
    )
    return (
        result.reshape(samples, rows_here, merged),
        grad_tokens.reshape(samples, rows_here, merged),
        summed[0],
        summed[1],
        summed[2],
        summed[3],
        summed[4],
        summed[5],
    )


def solution(mesh):
    return jax.shard_map(
        body,
        mesh=mesh,
        in_specs=(
            P(None, "lat", "ch"),
            P("ch"),
            P("ch"),
            P(None, "ch", None, None),
            P(None, "ch", None),
            P(None, "ch", None, None),
            P(None, "ch", None),
            P(None, "lat", "ch"),
        ),
        out_specs=(
            P(None, "lat", "ch"),
            P(None, "lat", "ch"),
            P(None, "ch", None, None),
            P(None, "ch", None),
            P(None, "ch", None, None),
            P(None, "ch", None),
            P("ch"),
            P("ch"),
        ),
        check_vma=False,
    )
```

profile of v0, /device:TPU:0, one launch (start us, length us, event | category | flops | bytes accessed | tf_op | source)
XLA Modules:
  0.0 1481.9 jit_solution(14718903141224642516)
XLA Ops:
  16.2 40.7 %reshape.415 = bf16[16,4,384,180]{3,2,0,1:T(8,128)(2,1)} reshape(bf16[16,4,69120]{2,0,1:T(8,128)(2,1)} %copy.245) | data formatting | bytes 17694720 | tf_op jit(solution)/shard_map/reshape | solution.py:134
  56.9 14.6 convert_bitcast_fusion
  85.6 11.3 copy.221
  96.9 39.0 %reshape.423 = f32[16,4,384,180]{3,2,0,1:T(8,128)} reshape(f32[16,4,69120]{2,0,1:T(8,128)} %copy.221) | data formatting | bytes 35389440 | tf_op jit(solution)/shard_map/convert_element_type | solution.py:126
  135.9 11.5 fusion.132
  147.4 22.8 %copy.225 = f32[16,4,384,180]{2,0,3,1:T(8,128)} copy(f32[16,4,384,180]{3,2,0,1:T(8,128)} %reshape.423) | data formatting | bytes 35389440 | tf_op jit(solution)/shard_map/convert_element_type | solution.py:126
  198.1 47.4 %all-to-all-done.2 = bf16[2,16,4,91,384]{4,2,3,0,1:T(4,128)(2,1)} async-done(((bf16[2,16,4,91,384]{4,2,3,0,1:T(4,128)(2,1)}), bf16[2,16,4,91,384]{4,2,3,0,1:T(4,128)(2,1)}, u32[]{:S(2)}, u32[]{:S(2)}) %all-to-all-start.2) | async-done | bytes 8945696 | tf_op jit(solution)/shard_map/all_to_all | solution.py:106
  245.6 39.2 %all-to-all-start = ((bf16[2,16,4,91,384]{4,2,3,0,1:T(4,128)(2,1)}), bf16[2,16,4,91,384]{4,2,3,0,1:T(4,128)(2,1)}, u32[]{:S(2)}, u32[]{:S(2)}) async-start(bf16[2,16,4,91,384]{4,2,3,0,1:T(4,128)(2,1)} %copy.233), calls=%async_computation | async-start | bytes 17891328 | tf_op jit(solution)/shard_map/all_to_all | solution.py:106
  294.2 15.0 %all_to_all.18 = bf16[2,1,64,91,384]{4,2,0,3,1:T(8,128)(2,1)} reshape(bf16[2,16,4,91,384]{4,2,1,0,3:T(4,128)(2,1)} %copy.250) | data formatting | bytes 17891328 | tf_op jit(solution)/shard_map/all_to_all | solution.py:106
  309.2 14.5 fusion.57
  323.7 25.4 %reshape.465 = f32[2,1,64,91,4,96]{5,4,2,0,3,1:T(4,128)} reshape(f32[2,1,64,91,384]{4,2,0,3,1:T(8,128)} %fusion.57) | data formatting | bytes 35782656 | tf_op jit(solution)/shard_map/transpose(jvp())/reshape | solution.py:92
  349.1 96.0 %all-to-all-done = bf16[2,16,4,91,384]{4,2,3,0,1:T(4,128)(2,1)} async-done(((bf16[2,16,4,91,384]{4,2,3,0,1:T(4,128)(2,1)}), bf16[2,16,4,91,384]{4,2,3,0,1:T(4,128)(2,1)}, u32[]{:S(2)}, u32[]{:S(2)}) %all-to-all-start) | async-done | bytes 8945696 | tf_op jit(solution)/shard_map/all_to_all | solution.py:106
  453.6 15.0 %reshape.426 = bf16[2,64,91,384,1]{3,1,0,2,4:T(8,128)(2,1)} reshape(bf16[2,16,4,91,384]{4,2,1,0,3:T(4,128)(2,1)} %copy.234) | data formatting | bytes 17891328 | tf_op jit(solution)/shard_map/reshape.2
  468.6 11.0 fusion.54
  479.6 25.5 %reshape.411 = f32[2,64,91,4,96]{4,3,1,0,2:T(4,128)} reshape(f32[2,1,64,91,384]{4,2,0,3,1:T(8,128)} %fusion.54) | data formatting | bytes 35782656 | tf_op jit(solution)/shard_map/reshape.4
  505.1 35.8 %fusion.32 = f32[4,2,96,64,91,1]{2,4,5,3,1,0:T(8,128)} fusion(f32[2,64,91,4,96,1]{4,3,1,0,2,5:T(4,128)} %bitcast.377, f32[1,2,4,96,96]{4,3,0,1,2:T(8,128)S(1)} %maximum_bitcast_fusion.1, f32[1,2,4,96,96]{4,3,0,1,2:T(8,128)S(1)} %bitcast.381), kind=kOutput, calls=%fused_computation.49 | convolution fusion | flops 5152849920 | bytes 36372480 | tf_op jit(solution)/shard_map/jvp(pbhknc,prncd->rbhknd)/dot_general | solution.py:39
  540.9 46.4 %fusion.133 = (f32[2,4,96]{2,0,1:T(2,128)}, f32[2,1,64,91,4,96]{5,3,2,0,4,1:T(8,128)}, f32[2,1,64,91,4,96]{5,3,2,0,4,1:T(8,128)}) fusion(f32[2,4,96]{2,0,1:T(2,128)S(1)} %copy.238, f32[2,1,64,91,4,96]{5,4,2,0,3,1:T(4,128)} %reshape.465, f32[1,2,4,96,96]{4,3,0,1,2:T(8,128)S(1)} %maximum_bitcast_fusion, f32[1,2,4,96,96]{4,3,0,1,2:T(8,128)S(1)} %bitcast.383, ...), kind=kOutput, calls=%fused_computation.194 | convolution fusion | flops 5251251200 | bytes 72164352 | tf_op jit(solution)/shard_map/jvp(pbhknc,prncd->rbhknd)/dot_general | solution.py:39
  587.3 41.5 %fusion.8 = (f32[4,2,96,1,64,91]{2,5,4,1,0,3:T(8,128)}, f32[4,64,91,2,96,1]{4,2,5,1,3,0:T(8,128)}) fusion(f32[4,2,96,64,91,1]{2,4,5,3,1,0:T(8,128)} %fusion.32, f32[4,2,96]{2,1,0:T(2,128)S(1)} %copy.247, f32[2,1,64,91,4,96]{5,3,2,0,4,1:T(8,128)} %get-tuple-element.65, f32[1,2,4,96,96]{4,3,0,1,2:T(8,128)S(1)} %maximum_bitcast_fusion, ...), kind=kOutput, calls=%fused_computation.16 | convolution fusion | flops 5260197888 | bytes 72158208 | tf_op jit(solution)/shard_map/transpose(jvp(pbhknc,prncd->rbhknd))/dot_general | solution.py:39
  628.8 23.1 %fusion.60 = f32[2,1,64,91,4,96]{5,3,0,2,4,1:T(8,128)} fusion(f32[4,2,96,1,64,91]{2,5,4,1,0,3:T(8,128)} %get-tuple-element.91, f32[1,2,4,96,96]{4,3,0,1,2:T(8,128)S(1)} %maximum_bitcast_fusion.1, f32[1,2,4,96,96]{4,3,0,1,2:T(8,128)S(1)} %bitcast.382), kind=kOutput, calls=%fused_computation.91 | convolution fusion | flops 5152849920 | bytes 36372480 | tf_op jit(solution)/shard_map/transpose(jvp(pbhknc,prncd->rbhknd))/dot_general | solution.py:39
  652.0 29.7 %copy.260 = f32[2,1,64,91,4,96]{5,4,2,3,0,1:T(4,128)} copy(f32[2,1,64,91,4,96]{5,3,0,2,4,1:T(8,128)} %fusion.60) | data formatting | bytes 35782656 | tf_op jit(solution)/shard_map/transpose(jvp(pbhknc,prncd->rbhknd))/transpose | solution.py:39
  681.7 24.7 %reshape.420 = f32[2,1,64,91,384]{4,2,3,0,1:T(8,128)} reshape(f32[2,1,64,91,4,96]{5,4,2,3,0,1:T(4,128)} %copy.260) | data formatting | bytes 35782656 | tf_op jit(solution)/shard_map/transpose(jvp())/reshape | solution.py:88
  706.4 11.4 fusion.48
  717.8 19.6 %copy.263 = bf16[2,1,64,91,384]{4,0,3,1,2:T(2,128)(2,1)} copy(bf16[2,1,64,91,384]{4,2,0,3,1:T(8,128)(2,1)S(1)} %fusion.48) | data formatting | bytes 17891328 | tf_op jit(solution)/shard_map/convert_element_type | solution.py:111
  737.4 39.0 %all-to-all-start.3 = ((bf16[2,1,64,91,384]{4,0,3,1,2:T(2,128)(2,1)}), bf16[2,1,64,91,384]{4,0,3,1,2:T(2,128)(2,1)}, u32[]{:S(2)}, u32[]{:S(2)}) async-start(bf16[2,1,64,91,384]{4,0,3,1,2:T(2,128)(2,1)} %copy.263), calls=%async_computation.3 | async-start | bytes 17891328 | tf_op jit(solution)/shard_map/all_to_all | solution.py:112
  776.4 29.5 %copy.327 = f32[2,1,64,91,4,96]{5,4,2,0,3,1:T(4,128)} copy(f32[2,1,64,91,4,96]{5,3,2,0,4,1:T(8,128)} %get-tuple-element.66) | data formatting | bytes 35782656 | tf_op jit(solution)/shard_map/reshape.20
  805.9 24.7 %reshape.435 = f32[2,64,91,384,1]{3,1,0,2,4:T(8,128)} reshape(f32[2,1,64,91,4,96]{5,4,2,0,3,1:T(4,128)} %copy.327) | data formatting | bytes 35782656 | tf_op jit(solution)/shard_map/reshape.20
  830.6 10.8 fusion.47
  841.5 19.6 %copy.241 = bf16[2,1,64,91,384]{4,0,3,1,2:T(2,128)(2,1)} copy(bf16[2,1,64,91,384]{4,2,0,3,1:T(8,128)(2,1)S(1)} %fusion.47) | data formatting | bytes 17891328 | tf_op jit(solution)/shard_map/convert_element_type | solution.py:111
  861.0 75.6 %all-to-all-done.3 = bf16[2,1,64,91,384]{4,0,3,1,2:T(2,128)(2,1)} async-done(((bf16[2,1,64,91,384]{4,0,3,1,2:T(2,128)(2,1)}), bf16[2,1,64,91,384]{4,0,3,1,2:T(2,128)(2,1)}, u32[]{:S(2)}, u32[]{:S(2)}) %all-to-all-start.3) | async-done | bytes 8945696 | tf_op jit(solution)/shard_map/all_to_all | solution.py:112
  936.6 38.8 %all-to-all-start.1 = ((bf16[2,1,64,91,384]{4,0,3,1,2:T(2,128)(2,1)}), bf16[2,1,64,91,384]{4,0,3,1,2:T(2,128)(2,1)}, u32[]{:S(2)}, u32[]{:S(2)}) async-start(bf16[2,1,64,91,384]{4,0,3,1,2:T(2,128)(2,1)} %copy.241), calls=%async_computation.1 | async-start | bytes 17891328 | tf_op jit(solution)/shard_map/all_to_all | solution.py:112
  975.5 15.9 %copy.246 = bf16[16,4,384,180]{2,0,3,1:T(8,128)(2,1)} copy(bf16[16,4,384,180]{3,2,0,1:T(8,128)(2,1)} %reshape.415) | data formatting | bytes 17694720 | tf_op jit(solution)/shard_map/reshape | solution.py:134
  991.4 29.6 %fusion.76 = f32[2,2,4,96,96]{3,4,0,1,2:T(8,128)S(1)} fusion(f32[2,4,96]{2,0,1:T(2,128)S(1)} %copy-done.27, f32[4,2,96,64,91,1]{2,4,5,3,1,0:T(8,128)} %fusion.32, f32[2,1,64,91,4,96]{5,3,2,0,4,1:T(8,128)} %get-tuple-element.65), kind=kOutput, calls=%fused_computation.95 | convolution fusion | flops 5192957952 | bytes 36375552 | tf_op jit(solution)/shard_map/transpose(jvp(pbhknc,prncd->rbhknd))/dot_general | solution.py:39
  1021.8 43.7 %fusion.71 = f32[2,2,4,96,96]{3,4,0,1,2:T(8,128)S(1)} fusion(f32[2,64,91,4,96,1]{4,3,1,0,2,5:T(4,128)} %bitcast.378, f32[4,2,96,1,64,91]{2,5,4,1,0,3:T(8,128)} %get-tuple-element.91), kind=kOutput, calls=%fused_computation.94 | convolution fusion | flops 5152702464 | bytes 36372480 | tf_op jit(solution)/shard_map/transpose(jvp(pbhknc,prncd->rbhknd))/dot_general | solution.py:39
  1066.5 25.9 %fusion.4 = f32[2,4,96]{2,0,1:T(2,128)S(1)} fusion(f32[4,64,91,2,96,1]{4,2,5,1,3,0:T(8,128)} %get-tuple-element.92, f32[4,2,96,64,91,1]{2,4,5,3,1,0:T(8,128)} %fusion.32, f32[2,4,96]{2,0,1:T(2,128)S(1)} %copy-done.27), kind=kLoop, calls=%fused_computation.12 | loop fusion | flops 111820032 | bytes 35788800 | tf_op jit(solution)/shard_map/transpose(jvp())/reduce_sum | solution.py:89
  1092.4 132.6 %all-reduce.16.cloned.1.call-done = (f32[2,4,96,96]{2,3,1,0:T(8,128)}, f32[2,4,96,96]{2,3,1,0:T(8,128)}) async-done(((f32[2,4,96,96]{2,3,1,0:T(8,128)}, f32[2,4,96,96]{2,3,1,0:T(8,128)}), (f32[2,4,96,96]{2,3,1,0:T(8,128)}, f32[2,4,96,96]{2,3,1,0:T(8,128)})) %all-reduce.16.cloned.1.call-update) | async-done | bytes 589840 | tf_op jit(solution)/shard_map/psum | solution.py:160
  1228.8 9.3 copy.264
  1238.1 9.7 convolution_bitcast_fusion
  1247.9 10.4 copy.407
  1258.3 16.3 %multiply_reduce_fusion.1 = (f32[384]{0:T(512)S(1)}, f32[16,4,180]{0,2,1:T(8,128)S(1)}, f32[16,4,180]{0,2,1:T(8,128)S(1)}, f32[384]{0:T(512)S(1)}) fusion(bf16[16,4,384,180]{2,0,3,1:T(8,128)(2,1)} %copy.407, bf16[16,4,384,180]{2,0,3,1:T(8,128)(2,1)} %copy.246, f32[16,4,384,180]{2,0,3,1:T(8,128)} %copy.225, f32[16,4,180]{0,2,1:T(8,128)S(1)} %copy-done.4, ...), kind=kLoop, calls=%fused_computation.67 | loop fusion | flops 53060352 | bytes 35578368 | tf_op jit(solution)/shard_map/reduce_sum | solution.py:147
  1276.2 9.3 copy.242
  1285.5 9.7 convolution_bitcast_fusion.1
  1295.2 10.3 copy.408
  1305.5 58.8 %all-reduce.8 = (f32[2,4,96]{2,0,1:T(2,128)S(1)}, f32[2,4,96]{2,0,1:T(2,128)S(1)}, f32[384]{0:T(512)}, f32[384]{0:T(512)}) all-reduce(f32[2,4,96]{2,0,1:T(2,128)S(1)} %fusion.4, f32[2,4,96]{2,0,1:T(2,128)S(1)} %copy-done.28, f32[384]{0:T(512)S(1)} %get-tuple-element.48, ...), channel_id=1, replica_groups=mesh['lat'=16,'ch'=2] {'lat'}, use_global_device_ids=true, to_apply=%region_10.11 | all-reduce | flops 2304 | bytes 18432 | tf_op jit(solution)/shard_map/psum | solution.py:160
  1367.6 26.2 %fusion.38 = (bf16[16,4,384,180]{2,0,3,1:T(8,128)(2,1)}, bf16[16,4,384,180]{2,0,3,1:T(8,128)(2,1)}) fusion(bf16[16,4,384,180]{2,0,3,1:T(8,128)(2,1)} %copy.246, bf16[16,4,384,180]{2,0,3,1:T(8,128)(2,1)} %copy.407, f32[16,4,384,180]{2,0,3,1:T(8,128)} %copy.225, f32[16,4,180]{0,2,1:T(8,128)S(1)} %copy.271, f32[16,4,180]{0,2,1:T(8,128)S(1)} %copy.268, ...), kind=kLoop, calls=%fused_computation.64 | loop fusion | flops 75202560 | bytes 70964736 | tf_op jit(solution)/shard_map/convert_element_type | solution.py:159
  1393.8 17.4 %copy.346 = bf16[16,4,384,180]{3,2,1,0:T(8,128)(2,1)} copy(bf16[16,4,384,180]{2,0,3,1:T(8,128)(2,1)} %get-tuple-element.67) | data formatting | bytes 17694720
  1411.3 23.1 %reshape.464 = bf16[16,4,69120]{2,1,0:T(4,128)(2,1)} reshape(bf16[16,4,384,180]{3,2,1,0:T(8,128)(2,1)} %copy.346) | data formatting | bytes 17694720
  1434.4 17.4 %copy.328 = bf16[16,4,384,180]{3,2,1,0:T(8,128)(2,1)} copy(bf16[16,4,384,180]{2,0,3,1:T(8,128)(2,1)} %get-tuple-element.68) | data formatting | bytes 17694720
  1451.8 23.1 %reshape.463 = bf16[16,4,69120]{2,1,0:T(4,128)(2,1)} reshape(bf16[16,4,384,180]{3,2,1,0:T(8,128)(2,1)} %copy.328) | data formatting | bytes 17694720
  (114 shorter events, 79.1 us)
Async XLA Ops:
  7.6 63.9 %copy-start.5 = (f32[1,91,180]{1,2,0:T(8,128)}, f32[1,91,180]{1,2,0:T(8,128)S(1)}, u32[]{:S(2)}) copy-start(f32[1,91,180]{1,2,0:T(8,128)S(1)} %get-tuple-element.89) | copy-start | bytes 196564
  7.6 63.9 %copy-start.7 = (f32[1,91,180]{1,2,0:T(8,128)}, f32[1,91,180]{1,2,0:T(8,128)S(1)}, u32[]{:S(2)}) copy-start(f32[1,91,180]{1,2,0:T(8,128)S(1)} %get-tuple-element.90) | copy-start | bytes 196564
  77.8 167.7 %all-to-all-start.2 = ((bf16[2,16,4,91,384]{4,2,3,0,1:T(4,128)(2,1)}), bf16[2,16,4,91,384]{4,2,3,0,1:T(4,128)(2,1)}, u32[]{:S(2)}, u32[]{:S(2)}) async-start(bf16[2,16,4,91,384]{4,2,3,0,1:T(4,128)(2,1)} %copy.249), calls=%async_computation.2 | async-start | bytes 17891328 | tf_op jit(solution)/shard_map/all_to_all | solution.py:106
  85.3 85.4 %all-reduce.20.cloned.1.call-start = ((), (), s32[]{:S(2)}) async-start(), calls=%async_computation.6 | async-start | bytes 262144 | tf_op jit(solution)/shard_map/psum | solution.py:101
  147.4 24.6 %copy-start.23 = (f32[384]{0:T(512)S(1)}, f32[384]{0:T(512)}, u32[]{:S(2)}) copy-start(f32[384]{0:T(512)} %param.9) | copy-start | bytes 4612
  147.4 24.6 %copy-start.30 = (f32[384]{0:T(512)S(1)}, f32[384]{0:T(512)}, u32[]{:S(2)}) copy-start(f32[384]{0:T(512)} %param.10) | copy-start | bytes 4612
  170.7 21.1 %copy-start.9 = (f32[1,180,91]{2,1,0:T(8,128)}, f32[1,180,91]{2,1,0:T(8,128)S(1)}, u32[]{:S(2)}) copy-start(f32[1,180,91]{2,1,0:T(8,128)S(1)} %get-tuple-element.93) | copy-start | bytes 196564
  170.7 21.1 %copy-start.11 = (f32[1,180,91]{2,1,0:T(8,128)}, f32[1,180,91]{2,1,0:T(8,128)S(1)}, u32[]{:S(2)}) copy-start(f32[1,180,91]{2,1,0:T(8,128)S(1)} %get-tuple-element.94) | copy-start | bytes 196564
  171.8 20.0 %copy-start.1 = (f32[16,4,180]{0,2,1:T(8,128)}, f32[16,4,180]{0,2,1:T(8,128)S(1)}, u32[]{:S(2)}) copy-start(f32[16,4,180]{0,2,1:T(8,128)S(1)} %copy.222) | copy-start | bytes 138244
  172.0 19.8 %copy-start.3 = (f32[16,4,180]{0,2,1:T(8,128)}, f32[16,4,180]{0,2,1:T(8,128)S(1)}, u32[]{:S(2)}) copy-start(f32[16,4,180]{0,2,1:T(8,128)S(1)} %copy.224) | copy-start | bytes 138244
  180.6 3.4 copy-start
  191.8 93.0 %copy-start.25 = (f32[2,4,96]{2,1,0:T(4,128)S(1)}, f32[2,4,96]{2,1,0:T(4,128)}, u32[]{:S(2)}) copy-start(f32[2,4,96]{2,1,0:T(4,128)} %param.12) | copy-start | bytes 9220
  191.8 93.0 %copy-start.29 = (f32[2,4,96]{2,1,0:T(4,128)S(1)}, f32[2,4,96]{2,1,0:T(4,128)}, u32[]{:S(2)}) copy-start(f32[2,4,96]{2,1,0:T(4,128)} %param.14) | copy-start | bytes 9220
  191.8 93.0 %copy-start.21 = (f32[2,4,96,96]{3,2,1,0:T(8,128)S(1)}, f32[2,4,96,96]{3,2,1,0:T(8,128)}, u32[]{:S(2)}) copy-start(f32[2,4,96,96]{3,2,1,0:T(8,128)} %param.11) | copy-start | bytes 884740
  191.8 93.0 %copy-start.22 = (f32[2,4,96,96]{3,2,1,0:T(8,128)S(1)}, f32[2,4,96,96]{3,2,1,0:T(8,128)}, u32[]{:S(2)}) copy-start(f32[2,4,96,96]{3,2,1,0:T(8,128)} %param.13) | copy-start | bytes 884740
  245.6 199.5 %all-to-all-start = ((bf16[2,16,4,91,384]{4,2,3,0,1:T(4,128)(2,1)}), bf16[2,16,4,91,384]{4,2,3,0,1:T(4,128)(2,1)}, u32[]{:S(2)}, u32[]{:S(2)}) async-start(bf16[2,16,4,91,384]{4,2,3,0,1:T(4,128)(2,1)} %copy.233), calls=%async_computation | async-start | bytes 17891328 | tf_op jit(solution)/shard_map/all_to_all | solution.py:106
  284.8 256.1 %copy-start.26 = (f32[2,4,96]{2,0,1:T(2,128)}, f32[2,4,96]{2,0,1:T(2,128)S(1)}, u32[]{:S(2)}) copy-start(f32[2,4,96]{2,0,1:T(2,128)S(1)} %copy.236) | copy-start | bytes 9220
  285.4 38.3 %copy-start.13 = (f32[1,2,64,64]{3,2,1,0:T(8,128)}, f32[1,2,64,64]{3,2,1,0:T(8,128)S(1)}, u32[]{:S(2)}) copy-start(f32[1,2,64,64]{3,2,1,0:T(8,128)S(1)} %get-tuple-element.85) | copy-start | bytes 98308
  285.4 38.3 %copy-start.15 = (f32[1,2,64,64]{3,2,1,0:T(8,128)}, f32[1,2,64,64]{3,2,1,0:T(8,128)S(1)}, u32[]{:S(2)}) copy-start(f32[1,2,64,64]{3,2,1,0:T(8,128)S(1)} %get-tuple-element.86) | copy-start | bytes 98308
  285.4 183.2 %copy-start.17 = (f32[1,2,64,64]{3,2,1,0:T(8,128)}, f32[1,2,64,64]{3,2,1,0:T(8,128)S(1)}, u32[]{:S(2)}) copy-start(f32[1,2,64,64]{3,2,1,0:T(8,128)S(1)} %get-tuple-element.87) | copy-start | bytes 98308
  285.5 183.2 %copy-start.19 = (f32[1,2,64,64]{3,2,1,0:T(8,128)}, f32[1,2,64,64]{3,2,1,0:T(8,128)S(1)}, u32[]{:S(2)}) copy-start(f32[1,2,64,64]{3,2,1,0:T(8,128)S(1)} %get-tuple-element.88) | copy-start | bytes 98308
  681.7 24.7 %copy-start.18 = (f32[1,2,64,64]{3,2,1,0:T(8,128)S(1)}, f32[1,2,64,64]{3,2,1,0:T(8,128)}, u32[]{:S(2)}) copy-start(f32[1,2,64,64]{3,2,1,0:T(8,128)} %copy-done.17) | copy-start | bytes 98308
  681.7 24.7 %copy-start.20 = (f32[1,2,64,64]{3,2,1,0:T(8,128)S(1)}, f32[1,2,64,64]{3,2,1,0:T(8,128)}, u32[]{:S(2)}) copy-start(f32[1,2,64,64]{3,2,1,0:T(8,128)} %copy-done.19) | copy-start | bytes 98308
  737.4 199.3 %all-to-all-start.3 = ((bf16[2,1,64,91,384]{4,0,3,1,2:T(2,128)(2,1)}), bf16[2,1,64,91,384]{4,0,3,1,2:T(2,128)(2,1)}, u32[]{:S(2)}, u32[]{:S(2)}) async-start(bf16[2,1,64,91,384]{4,0,3,1,2:T(2,128)(2,1)} %copy.263), calls=%async_computation.3 | async-start | bytes 17891328 | tf_op jit(solution)/shard_map/all_to_all | solution.py:112
  805.9 24.7 %copy-start.14 = (f32[1,2,64,64]{3,2,1,0:T(8,128)S(1)}, f32[1,2,64,64]{3,2,1,0:T(8,128)}, u32[]{:S(2)}) copy-start(f32[1,2,64,64]{3,2,1,0:T(8,128)} %copy-done.13) | copy-start | bytes 98308
  805.9 24.7 %copy-start.16 = (f32[1,2,64,64]{3,2,1,0:T(8,128)S(1)}, f32[1,2,64,64]{3,2,1,0:T(8,128)}, u32[]{:S(2)}) copy-start(f32[1,2,64,64]{3,2,1,0:T(8,128)} %copy-done.15) | copy-start | bytes 98308
  841.5 149.9 %copy-start.27 = (f32[2,4,96]{2,0,1:T(2,128)S(1)}, f32[2,4,96]{2,0,1:T(2,128)}, u32[]{:S(2)}) copy-start(f32[2,4,96]{2,0,1:T(2,128)} %copy-done.26) | copy-start | bytes 9220
  936.6 339.5 %all-to-all-start.1 = ((bf16[2,1,64,91,384]{4,0,3,1,2:T(2,128)(2,1)}), bf16[2,1,64,91,384]{4,0,3,1,2:T(2,128)(2,1)}, u32[]{:S(2)}, u32[]{:S(2)}) async-start(bf16[2,1,64,91,384]{4,0,3,1,2:T(2,128)(2,1)} %copy.241), calls=%async_computation.1 | async-start | bytes 17891328 | tf_op jit(solution)/shard_map/all_to_all | solution.py:112
  975.4 249.5 %all-reduce.16.cloned.1.call-start = ((), (), s32[]{:S(2)}) async-start(), calls=%async_computation.4 | async-start | bytes 1572864 | tf_op jit(solution)/shard_map/psum | solution.py:160
  1066.5 299.1 %all-reduce.18.cloned.1.call-start = ((), (), s32[]{:S(2)}) async-start(), calls=%async_computation.5 | async-start | bytes 262144 | tf_op jit(solution)/shard_map/psum | solution.py:101
  1066.5 171.6 %copy-start.10 = (f32[1,180,91]{2,1,0:T(8,128)S(1)}, f32[1,180,91]{2,1,0:T(8,128)}, u32[]{:S(2)}) copy-start(f32[1,180,91]{2,1,0:T(8,128)} %copy-done.9) | copy-start | bytes 196564
  1066.5 171.6 %copy-start.12 = (f32[1,180,91]{2,1,0:T(8,128)S(1)}, f32[1,180,91]{2,1,0:T(8,128)}, u32[]{:S(2)}) copy-start(f32[1,180,91]{2,1,0:T(8,128)} %copy-done.11) | copy-start | bytes 196564
  1238.1 20.2 %copy-start.2 = (f32[16,4,180]{0,2,1:T(8,128)S(1)}, f32[16,4,180]{0,2,1:T(8,128)}, u32[]{:S(2)}) copy-start(f32[16,4,180]{0,2,1:T(8,128)} %copy-done.1) | copy-start | bytes 138244
  1238.1 20.2 %copy-start.4 = (f32[16,4,180]{0,2,1:T(8,128)S(1)}, f32[16,4,180]{0,2,1:T(8,128)}, u32[]{:S(2)}) copy-start(f32[16,4,180]{0,2,1:T(8,128)} %copy-done.3) | copy-start | bytes 138244
  1238.1 20.2 %copy-start.24 = (f32[384]{0:T(512)S(1)}, f32[384]{0:T(512)}, u32[]{:S(2)}) copy-start(f32[384]{0:T(512)} %param.9) | copy-start | bytes 4612
  1258.3 27.2 %copy-start.6 = (f32[1,91,180]{1,2,0:T(8,128)S(1)}, f32[1,91,180]{1,2,0:T(8,128)}, u32[]{:S(2)}) copy-start(f32[1,91,180]{1,2,0:T(8,128)} %copy-done.5) | copy-start | bytes 196564
  1258.3 27.2 %copy-start.8 = (f32[1,91,180]{1,2,0:T(8,128)S(1)}, f32[1,91,180]{1,2,0:T(8,128)}, u32[]{:S(2)}) copy-start(f32[1,91,180]{1,2,0:T(8,128)} %copy-done.7) | copy-start | bytes 196564
  1285.5 20.0 %copy-start.28 = (f32[2,4,96]{2,0,1:T(2,128)S(1)}, f32[2,4,96]{2,0,1:T(2,128)}, u32[]{:S(2)}) copy-start(f32[2,4,96]{2,0,1:T(2,128)} %get-tuple-element.64) | copy-start | bytes 9220
Sparse Core Ops, SparseCore 0:
  147.5 22.8 all-reduce.19
  1066.6 158.3 all-reduce.15
  1276.3 20.5 all-reduce.17
where the time goes:
time: 1500 us; the launch traced here: 1480 us
  local copies, waits for them, and re-layouts  528 us (35%)
  waiting for transfers between devices  352 us (23%)
  matrix products  310 us (21%)
  starting transfers between devices  125 us (8%)
  other arithmetic  94.1 us (6%)
  blocking collectives  58.8 us (4%)
    dot_general x14, matrix products, contract(): return jnp.einsum(spec, left, right, precision=fast)  310 us
    all_to_all x2, waiting for transfers between devices, spectra_columns(): moved = lax.all_to_all(sent, 'lat', split_axis=1, concat_axis=2, tiled=True)  143 us
    psum x1, waiting for transfers between devices, body(): lax.psum((param_grads[0], param_grads[1], param_grads[2], param_grads[3],...  133 us
    unnamed x75, local copies, waits for them, and re-layouts  98.3 us
    another operation x4, local copies, waits for them, and re-layouts  94.7 us
    all_to_all x2, starting transfers between devices, spectra_rows(): moved = lax.all_to_all(sent, 'lat', split_axis=2, concat_axis=1, tiled=True)  77.8 us
    all_to_all x2, waiting for transfers between devices, spectra_rows(): moved = lax.all_to_all(sent, 'lat', split_axis=2, concat_axis=1, tiled=True)  75.6 us
    convert_element_type x3, local copies, waits for them, and re-layouts, body(): as_float = tokens.reshape(field_shape).astype(jnp.float32)  73.2 us
  transfers between devices with their start and end apart: 7, of which 4 were waited for; matrix products, arithmetic and copies ran while one was open for 30% of the time, Pallas kernels for 0%

commit v1 on v0

v1 whole, which is shorter than its diff:
```python
import functools
import math

import jax
import jax.numpy as jnp
import numpy as np
from jax import lax
from jax.experimental import pallas as pl
from jax.experimental.pallas import tpu as pltpu
from jax.sharding import PartitionSpec as P

layer_eps = 1e-05
shrink_level = 0.1
LANE = 128
PAD = 256
F32 = jnp.float32
BF16 = jnp.bfloat16
GELU_SCALE = math.sqrt(2.0 / math.pi)
GELU_CUBE = 0.044715
VMEM_BYTES = 60 * 1024 * 1024


def split_table(table):
    full = jnp.asarray(table, F32)
    high = lax.reduce_precision(full, 8, 7)
    return high.astype(BF16), (full - high).astype(BF16)


def left_table(table, passes):
    high, low = split_table(table)
    return jnp.concatenate((high, high, low)[:passes] if passes != 2 else (high, low), axis=1)


def right_table(table, passes):
    high, low = split_table(table)
    return jnp.concatenate((high, high, low)[:passes] if passes != 2 else (high, low), axis=0)


def latitude_table(height):
    cells = np.arange(height)
    table = np.zeros((height, height))
    for pair in range(height // 2):
        angle = 2.0 * np.pi * (pair * cells % height) / height
        table[2 * pair] = np.cos(angle)
        table[2 * pair + 1] = -np.sin(angle)
    table[1] = np.cos(np.pi * cells)
    return table


def longitude_table(width):
    modes = width // 2 + 1
    cells = np.arange(width)[:, None]
    angle = 2.0 * np.pi * (cells * np.arange(modes)[None] % width) / width
    table = np.zeros((PAD, PAD))
    table[:width, :modes] = np.cos(angle)
    table[:width, LANE : LANE + modes] = -np.sin(angle)
    doubled = np.full((modes,), 2.0)
    doubled[0] = 1.0
    if width % 2 == 0:
        doubled[-1] = 1.0
    weights = np.zeros((PAD,))
    weights[:modes] = doubled
    weights[LANE : LANE + modes] = doubled
    return table, table * weights[None]


def dot(left, right):
    return jnp.dot(left, right, preferred_element_type=F32)


def dot_rows(left, right):
    return lax.dot_general(left, right, (((1,), (1,)), ((), ())), preferred_element_type=F32)


def pair_forward(values, first, half):
    real_cos = values[:half, :LANE]
    real_sin = values[:half, LANE:]
    imag_cos = values[half:, :LANE]
    imag_sin = values[half:, LANE:]
    re_left = jnp.where(first, real_cos, real_cos - imag_sin)
    re_right = jnp.where(first, imag_cos, real_cos + imag_sin)
    im_left = jnp.where(first, real_sin, imag_cos + real_sin)
    im_right = jnp.where(first, imag_sin, real_sin - imag_cos)
    top = jnp.concatenate((re_left, re_right), axis=1)
    bottom = jnp.concatenate((im_left, im_right), axis=1)
    return jnp.concatenate((top, bottom), axis=0)


def pair_inverse(values, first, half):
    re_left = values[:half, :LANE]
    re_right = values[:half, LANE:]
    im_left = values[half:, :LANE]
    im_right = values[half:, LANE:]
    a = jnp.where(first, re_left, re_left + re_right)
    b = jnp.where(first, im_left, im_left + im_right)
    c = jnp.where(first, re_right, im_left - im_right)
    d = jnp.where(first, im_right, re_right - re_left)
    top = jnp.concatenate((a, b), axis=1)
    bottom = jnp.concatenate((c, d), axis=1)
    return jnp.concatenate((top, bottom), axis=0)


def split(values):
    high = values.astype(BF16)
    return high, (values - high.astype(F32)).astype(BF16)


def to_modes(x_ref, lat_ref, flat, low, high, group, width, block):
    height = x_ref.shape[0]
    span = group * width
    flat[:, span:] = jnp.zeros((height, flat.shape[1] - span), F32)

    def one(step, carry):
        at = pl.multiple_of(step * span, LANE)
        piece = x_ref[:, pl.ds(at, span)]
        if lat_ref.shape[1] == 2 * height:
            piece = jnp.concatenate((piece, piece), axis=0)
        flat[:, :span] = dot(lat_ref[...], piece)
        for channel in range(group):
            start = channel * width
            rows = pl.ds(step * group + channel, height, stride=block)
            low[rows, :] = flat[:, start : start + LANE]
            high[rows, :] = flat[:, start + LANE : start + PAD]
        return carry

    lax.fori_loop(0, block // group, one, 0)


def from_modes(out_ref, lat_ref, flat, low, high, group, width, block):
    height = out_ref.shape[0]
    span = group * width

    def one(step, carry):
        at = pl.multiple_of(step * span, LANE)
        for channel in range(group):
            start = channel * width
            rows = pl.ds(step * group + channel, height, stride=block)
            flat[:, start : start + LANE] = low[rows, :]
            flat[:, start + LANE : start + PAD] = high[rows, :]
        piece = flat[:, :span].astype(BF16)
        out = dot(lat_ref[...], piece) * (1.0 / math.sqrt(height * width))
        out_ref[:, pl.ds(at, span)] = out.astype(BF16)
        return carry

    lax.fori_loop(0, block // group, one, 0)


def load_rows(low, high, rows):
    return jnp.concatenate((low[rows, :], high[rows, :]), axis=1)


def forward_kernel(
    group, width, block, unroll, x_ref, lat_ref, lat_back_ref, lon_ref, lon_back_ref, first_ref,
    first_bias_ref, second_ref, second_bias_ref, out_ref, spec_ref, slope_ref, hidden_ref,
    shrink_ref, flat, low, high,
):
    height = x_ref.shape[0]
    to_modes(x_ref, lat_ref, flat, low, high, group, width, block)
    two = 2 * block

    def one(step, carry):
        rows = pl.ds(pl.multiple_of(step * (unroll * two), 8), unroll * two)
        major, minor = split(load_rows(low, high, rows))
        modes = dot(jnp.concatenate((major, minor, major), axis=1), lon_ref[...])
        backs = []
        for index in range(unroll):
            pair = step * unroll + index
            first = pair == 0
            major, minor = split(pair_forward(modes[index * two : (index + 1) * two], first, block))
            spec_ref[0, pair] = major
            pre = dot(first_ref[0], jnp.concatenate((major, minor, major), axis=0))
            pre = pre + first_bias_ref[0]
            square = pre * pre
            inner = jnp.tanh(GELU_SCALE * (pre + GELU_CUBE * square * pre))
            half = 0.5 * (1.0 + inner)
            slope = half + 0.5 * GELU_SCALE * pre * (1.0 - inner * inner) * (
                1.0 + 3.0 * GELU_CUBE * square
            )
            slope_ref[0, pair] = slope.astype(BF16)
            major, minor = split(pre * half)
            hidden_ref[0, pair] = major
            mixed = dot(second_ref[0], jnp.concatenate((major, minor, major), axis=0))
            mixed = mixed + second_bias_ref[0]
            shrink = jnp.tanh(mixed / shrink_level)
            shrink_ref[0, pair] = (shrink * shrink).astype(BF16)
            mixed = mixed - shrink_level * shrink
            backs.append(pair_inverse(mixed, first, block).astype(BF16))
        back = dot(jnp.concatenate(backs, axis=0), lon_back_ref[...])
        low[rows, :] = back[:, :LANE]
        high[rows, :] = back[:, LANE:]
        return carry

    lax.fori_loop(0, height // (2 * unroll), one, 0)
    from_modes(out_ref, lat_back_ref, flat, low, high, group, width, block)


def backward_kernel(
    group, width, block, unroll, x_ref, spec_ref, slope_ref, hidden_ref, shrink_ref, lat_ref,
    lat_back_ref, lon_ref, lon_back_ref, first_ref, second_ref, out_ref, first_grad_ref,
    first_bias_grad_ref, second_grad_ref, second_bias_grad_ref, flat, low, high,
):
    height = x_ref.shape[0]
    to_modes(x_ref, lat_ref, flat, low, high, group, width, block)
    two = 2 * block
    first_grad_ref[...] = jnp.zeros_like(first_grad_ref)
    second_grad_ref[...] = jnp.zeros_like(second_grad_ref)
    first_bias_grad_ref[...] = jnp.zeros_like(first_bias_grad_ref)
    second_bias_grad_ref[...] = jnp.zeros_like(second_bias_grad_ref)

    def one(step, carry):
        rows = pl.ds(pl.multiple_of(step * (unroll * two), 8), unroll * two)
        modes = dot(load_rows(low, high, rows).astype(BF16), lon_ref[...])
        backs = []
        grads = []
        for index in range(unroll):
            pair = step * unroll + index
            first = pair == 0
            grad = pair_forward(modes[index * two : (index + 1) * two], first, block)
            outer = grad * shrink_ref[0, pair].astype(F32)
            outer_low = outer.astype(BF16)
            inner = dot(second_ref[0], outer_low) * slope_ref[0, pair].astype(F32)
            inner_low = inner.astype(BF16)
            back = pair_inverse(dot(first_ref[0], inner_low), first, block)
            backs.append(back.astype(BF16))
            grads.append((outer, outer_low, inner, inner_low))
        hiddens = jnp.concatenate([hidden_ref[0, step * unroll + i] for i in range(unroll)], axis=1)
        specs = jnp.concatenate([spec_ref[0, step * unroll + i] for i in range(unroll)], axis=1)
        outers = jnp.concatenate([grad[1] for grad in grads], axis=1)
        inners = jnp.concatenate([grad[3] for grad in grads], axis=1)
        second_grad_ref[0] += dot_rows(outers, hiddens)
        first_grad_ref[0] += dot_rows(inners, specs)
        outer_sum = sum(grad[0][:, :LANE] + grad[0][:, LANE:] for grad in grads)
        inner_sum = sum(grad[2][:, :LANE] + grad[2][:, LANE:] for grad in grads)
        second_bias_grad_ref[0] += outer_sum
        first_bias_grad_ref[0] += inner_sum
        back = dot(jnp.concatenate(backs, axis=0), lon_back_ref[...])
        low[rows, :] = back[:, :LANE]
        high[rows, :] = back[:, LANE:]
        return carry

    lax.fori_loop(0, height // (2 * unroll), one, 0)
    from_modes(out_ref, lat_back_ref, flat, low, high, group, width, block)


def whole(array):
    rank = array.ndim
    return pl.BlockSpec(array.shape, lambda *_: (0,) * rank)


def per_block(shape, offset=0):
    rank = len(shape)
    return pl.BlockSpec((1,) + tuple(shape), lambda n: (n + offset,) + (0,) * rank)


def column_scratch(height, group, width, block):
    return [
        pltpu.VMEM((height, group * width + LANE), F32),
        pltpu.VMEM((height * block, LANE), F32),
        pltpu.VMEM((height * block, LANE), F32),
    ]


def column_forward(x, tables, params, group, width, block, start, unroll=4):
    height, lanes = x.shape
    blocks = lanes // (block * width)
    pairs = height // 2
    two = 2 * block
    wide = pl.BlockSpec((height, block * width), lambda n: (0, n))
    kept = per_block((pairs, two, PAD))
    cells = blocks * pairs * two * PAD
    return pl.pallas_call(
        functools.partial(forward_kernel, group, width, block, unroll),
        grid=(blocks,),
        in_specs=[
            wide, *[whole(table) for table in tables],
            per_block((two, 3 * two), start), per_block((two, 1), start),
            per_block((two, 3 * two), start), per_block((two, 1), start),
        ],
        out_specs=[wide] + [kept] * 4,
        out_shape=[jax.ShapeDtypeStruct(x.shape, BF16)]
        + [jax.ShapeDtypeStruct((blocks, pairs, two, PAD), BF16)] * 4,
        scratch_shapes=column_scratch(height, group, width, block),
        compiler_params=pltpu.CompilerParams(vmem_limit_bytes=VMEM_BYTES),
        cost_estimate=pl.CostEstimate(
            flops=cells * 20000, bytes_accessed=4 * height * lanes + 8 * cells, transcendentals=0
        ),
        name="column_forward",
    )(x, *tables, *params)


def column_backward(x, kept_arrays, tables, params, group, width, block, start, local, unroll=4):
    height, lanes = x.shape
    blocks = lanes // (block * width)
    pairs = height // 2
    two = 2 * block
    wide = pl.BlockSpec((height, block * width), lambda n: (0, n))
    kept = per_block((pairs, two, PAD), local)
    cells = blocks * pairs * two * PAD
    sizes = ((two, two), (two, LANE)) * 2
    return pl.pallas_call(
        functools.partial(backward_kernel, group, width, block, unroll),
        grid=(blocks,),
        in_specs=[
            wide, kept, kept, kept, kept, *[whole(table) for table in tables],
            per_block((two, two), start), per_block((two, two), start),
        ],
        out_specs=[wide] + [per_block(size) for size in sizes],
        out_shape=[jax.ShapeDtypeStruct(x.shape, BF16)]
        + [jax.ShapeDtypeStruct((blocks,) + size, F32) for size in sizes],
        scratch_shapes=column_scratch(height, group, width, block),
        compiler_params=pltpu.CompilerParams(vmem_limit_bytes=VMEM_BYTES),
        cost_estimate=pl.CostEstimate(
            flops=cells * 20000, bytes_accessed=4 * height * lanes + 8 * cells, transcendentals=0
        ),
        name="column_backward",
    )(x, *kept_arrays, *tables, *params)


def fold(acc, group, width):
    total = acc[:, :width]
    for channel in range(1, group):
        total = total + acc[:, channel * width : (channel + 1) * width]
    return total


def spread(wide, token, group, width):
    for channel in range(group):
        wide[:, channel * width : (channel + 1) * width] = token


def each_group(groups, span, step_body):
    def one(step, carry):
        step_body(pl.ds(pl.multiple_of(step * span, LANE), span))
        return carry

    lax.fori_loop(0, groups, one, 0)


def stats_kernel(group, width, x_ref, total_ref, square_ref, acc, acc_square):
    span = group * width
    acc[...] = jnp.zeros_like(acc)
    acc_square[...] = jnp.zeros_like(acc_square)

    def one(at):
        piece = x_ref[0, :, at].astype(F32)
        acc[...] += piece
        acc_square[...] += piece * piece

    each_group(x_ref.shape[2] // span, span, one)
    total_ref[0] = fold(acc, group, width)
    square_ref[0] = fold(acc_square, group, width)


def norm_kernel(group, width, x_ref, center_ref, inv_ref, gain_ref, shift_ref, out_ref, center, inv):
    span = group * width
    spread(center, center_ref[0], group, width)
    spread(inv, inv_ref[0], group, width)

    def one(at):
        standard = (x_ref[0, :, at].astype(F32) - center[...]) * inv[...]
        out_ref[0, :, at] = (standard * gain_ref[:, at] + shift_ref[:, at]).astype(BF16)

    each_group(x_ref.shape[2] // span, span, one)


def sums_kernel(
    group, width, x_ref, up_ref, grad_ref, center_ref, inv_ref, gain_ref,
    mean_ref, cross_ref, gain_grad_ref, shift_grad_ref, center, inv, acc, acc_cross,
):
    span = group * width
    spread(center, center_ref[0], group, width)
    spread(inv, inv_ref[0], group, width)
    acc[...] = jnp.zeros_like(acc)
    acc_cross[...] = jnp.zeros_like(acc_cross)

    @pl.when(pl.program_id(0) == 0)
    def _():
        gain_grad_ref[...] = jnp.zeros_like(gain_grad_ref)
        shift_grad_ref[...] = jnp.zeros_like(shift_grad_ref)

    def one(at):
        standard = (x_ref[0, :, at].astype(F32) - center[...]) * inv[...]
        grad = up_ref[0, :, at].astype(F32) + grad_ref[0, :, at].astype(F32)
        product = grad * standard
        gain_grad_ref[:, at] += product
        shift_grad_ref[:, at] += grad
        gain = gain_ref[:, at]
        acc[...] += grad * gain
        acc_cross[...] += product * gain

    each_group(x_ref.shape[2] // span, span, one)
    mean_ref[0] = fold(acc, group, width)
    cross_ref[0] = fold(acc_cross, group, width)


def final_kernel(
    group, width, x_ref, up_ref, grad_ref, center_ref, inv_ref, mean_ref, cross_ref, gain_ref,
    out_ref, center, inv, mean, cross,
):
    span = group * width
    spread(center, center_ref[0], group, width)
    spread(inv, inv_ref[0], group, width)
    spread(mean, mean_ref[0], group, width)
    spread(cross, cross_ref[0], group, width)

    def one(at):
        standard = (x_ref[0, :, at].astype(F32) - center[...]) * inv[...]
        up = up_ref[0, :, at].astype(F32)
        grad = (up + grad_ref[0, :, at].astype(F32)) * gain_ref[:, at]
        out = up + inv[...] * (grad - mean[...] - standard * cross[...])
        out_ref[0, :, at] = out.astype(BF16)

    each_group(x_ref.shape[2] // span, span, one)


def result_kernel(x_ref, normed_ref, filtered_ref, out_ref):
    out = x_ref[...].astype(F32) + normed_ref[...].astype(F32) + filtered_ref[...].astype(F32)
    out_ref[...] = out.astype(BF16)


def row_call(kernel, name, inputs, kinds, out_kinds, sizes, scratch):
    samples, rows_here, lanes, width = sizes
    shapes = {
        "field": (samples, rows_here, lanes),
        "token": (samples, rows_here, width),
        "lane": (1, lanes),
        "sum": (rows_here, lanes),
    }
    specs = {
        "field": pl.BlockSpec((1, rows_here, lanes), lambda b: (b, 0, 0)),
        "token": pl.BlockSpec((1, rows_here, width), lambda b: (b, 0, 0)),
        "lane": pl.BlockSpec((1, lanes), lambda b: (0, 0)),
        "sum": pl.BlockSpec((rows_here, lanes), lambda b: (0, 0)),
    }
    cells = samples * rows_here * lanes
    return pl.pallas_call(
        kernel,
        grid=(samples,),
        in_specs=[specs[kind] for kind in kinds],
        out_specs=[specs[kind] for kind in out_kinds],
        out_shape=[
            jax.ShapeDtypeStruct(shapes[kind], BF16 if kind == "field" else F32)
            for kind in out_kinds
        ],
        scratch_shapes=scratch,
        compiler_params=pltpu.CompilerParams(vmem_limit_bytes=VMEM_BYTES),
        cost_estimate=pl.CostEstimate(
            flops=cells * 2000, bytes_accessed=2 * cells * (len(kinds) + 1), transcendentals=0
        ),
        name=name,
    )(*inputs)


def swap(values):
    return lax.all_to_all(values, "lat", split_axis=0, concat_axis=0, tiled=True)


def channel_sum(first, second, ch):
    both = jnp.stack((first, second))
    if ch == 2:
        both = both + lax.ppermute(both, "ch", [(0, 1), (1, 0)])
    else:
        both = lax.psum(both, "ch")
    return both[0], both[1]


def wide_matrix(matrix):
    high, low = split_table(matrix)
    return jnp.concatenate((high, high, low), axis=2)


def real_matrix(weight):
    turned = jnp.swapaxes(weight, 2, 3)
    top = jnp.concatenate((turned[0], -turned[1]), axis=2)
    bottom = jnp.concatenate((turned[1], turned[0]), axis=2)
    return jnp.concatenate((top, bottom), axis=1)


def weight_grad(grad, block):
    same = grad[:, :block, :block] + grad[:, block:, block:]
    other = grad[:, block:, :block] - grad[:, :block, block:]
    return jnp.swapaxes(jnp.stack((same, other)), 2, 3)


def bias_rows(bias):
    return jnp.concatenate((bias[0], bias[1]), axis=1)[:, :, None]


def bias_grad(grad, block):
    total = jnp.sum(grad, axis=2)
    return jnp.stack((total[:, :block], total[:, block:]))


def body(
    lat, ch, embed, tokens, norm_gain, norm_shift, first_weight, first_bias, second_weight, second_bias, upstream
):
    samples, rows_here, lanes = tokens.shape
    channels = norm_gain.shape[0]
    width = lanes // channels
    height = rows_here * lat
    block = first_weight.shape[2]
    blocks = first_weight.shape[1]
    group = LANE // math.gcd(width, LANE)
    span = group * width
    sizes = (samples, rows_here, lanes, width)
    lat_table = latitude_table(height)
    lon_table, lon_weighted = longitude_table(width)
    lat_forward = left_table(lat_table / math.sqrt(height * width), 2)
    lat_back = left_table(lat_table.T, 1)
    forward_tables = (lat_forward, lat_back, right_table(lon_table, 3), right_table(lon_weighted.T, 1))
    backward_tables = (lat_forward, lat_back, right_table(lon_weighted, 1), right_table(lon_table.T, 1))
    first = real_matrix(first_weight)
    second = real_matrix(second_weight)
    forward_params = (
        wide_matrix(first), bias_rows(first_bias), wide_matrix(second), bias_rows(second_bias),
    )
    backward_params = (
        jnp.swapaxes(first, 1, 2).astype(BF16), jnp.swapaxes(second, 1, 2).astype(BF16),
    )
    gain_lanes = jnp.repeat(norm_gain, width)[None]
    shift_lanes = jnp.repeat(norm_shift, width)[None]
    wide = pltpu.VMEM((rows_here, span), F32)

    early = blocks // 4 * block * width
    upstream_columns = []
    if early:
        upstream_columns.append(swap(upstream[:, :, :early]))
    totals, squares = row_call(
        functools.partial(stats_kernel, group, width), "stats", (tokens,), ("field",),
        ("token", "token"), sizes, [wide, wide],
    )
    totals, squares = channel_sum(totals, squares, ch)
    center = totals / embed
    variance = squares / embed - center * center
    inv_scale = lax.rsqrt(variance + layer_eps)
    (normed,) = row_call(
        functools.partial(norm_kernel, group, width), "norm",
        (tokens, center, inv_scale, gain_lanes, shift_lanes),
        ("field", "token", "token", "lane", "lane"), ("field",), sizes, [wide, wide],
    )
    sent = normed
    if early:
        sent, upstream_columns[0] = lax.optimization_barrier((normed, upstream_columns[0]))
    normed_columns = swap(sent)
    rest, normed_columns = lax.optimization_barrier((upstream[:, :, early:], normed_columns))
    upstream_columns.append(swap(rest))
    filtered, *kept = column_forward(
        normed_columns.reshape(height, lanes), forward_tables, forward_params, group, width, block, 0
    )
    filtered, upstream_columns[-1] = lax.optimization_barrier(
        (filtered.reshape(lat, rows_here, lanes), upstream_columns[-1])
    )
    filtered_rows = swap(filtered)
    spectral, first_grad, first_bias_grad, second_grad, second_bias_grad = column_backward(
        jnp.concatenate(upstream_columns, axis=2).reshape(height, lanes), kept,
        backward_tables, backward_params, group, width, block, 0, 0,
    )
    spectral, filtered_rows = lax.optimization_barrier(
        (spectral.reshape(lat, rows_here, lanes), filtered_rows)
    )
    spectral_rows = swap(spectral)
    (result,) = row_call(
        result_kernel, "result", (tokens, normed, filtered_rows), ("field",) * 3, ("field",), sizes, [],
    )
    first_all = jnp.concatenate(
        (weight_grad(first_grad, block), bias_grad(first_bias_grad, block)[:, :, None]), axis=2
    )
    second_all = jnp.concatenate(
        (weight_grad(second_grad, block), bias_grad(second_bias_grad, block)[:, :, None]), axis=2
    )
    first_all, second_all = lax.psum((first_all, second_all), "lat")
    spectral_rows, result, first_all, second_all = lax.optimization_barrier(
        (spectral_rows, result, first_all, second_all)
    )
    mean, cross, gain_part, shift_part = row_call(
        functools.partial(sums_kernel, group, width), "sums",
        (tokens, upstream, spectral_rows, center, inv_scale, gain_lanes),
        ("field", "field", "field", "token", "token", "lane"),
        ("token", "token", "sum", "sum"), sizes, [wide] * 4,
    )
    gain_part = jnp.sum(gain_part.reshape(rows_here, channels, width), axis=(0, 2))
    shift_part = jnp.sum(shift_part.reshape(rows_here, channels, width), axis=(0, 2))
    mean, cross = channel_sum(mean, cross, ch)
    (grad_tokens,) = row_call(
        functools.partial(final_kernel, group, width), "final",
        (tokens, upstream, spectral_rows, center, inv_scale, mean / embed, cross / embed, gain_lanes),
        ("field", "field", "field", "token", "token", "token", "token", "lane"),
        ("field",), sizes, [wide] * 4,
    )
    vector = jnp.stack((gain_part, shift_part))[None]
    vector = jnp.broadcast_to(vector, (lat, 2, channels))
    gain_grad, shift_grad = jnp.sum(swap(vector), axis=0)
    return (
        result, grad_tokens, first_all[:, :, :block], first_all[:, :, block],
        second_all[:, :, :block], second_all[:, :, block], gain_grad, shift_grad,
    )


def solution(mesh):
    lat = mesh.shape["lat"]
    ch = mesh.shape["ch"]

    def step(tokens, norm_gain, *rest):
        return jax.shard_map(
            functools.partial(body, lat, ch, norm_gain.shape[0]),
            mesh=mesh,
            in_specs=(
                P(None, "lat", "ch"),
                P("ch"),
                P("ch"),
                P(None, "ch", None, None),
                P(None, "ch", None),
                P(None, "ch", None, None),
                P(None, "ch", None),
                P(None, "lat", "ch"),
            ),
            out_specs=(
                P(None, "lat", "ch"),
                P(None, "lat", "ch"),
                P(None, "ch", None, None),
                P(None, "ch", None),
                P(None, "ch", None, None),
                P(None, "ch", None),
                P("ch"),
                P("ch"),
            ),
            check_vma=False,
        )(tokens, norm_gain, *rest)

    return step
```

time: 1500 us -> 937 us (0.62)
  local copies, waits for them, and re-layouts: 528 us -> 69.7 us
  Pallas kernels: 0 us -> 324 us
  matrix products: 310 us -> 0 us
  other arithmetic: 94.1 us -> 23.4 us
  blocking collectives: 58.8 us -> 0 us
  waiting for transfers between devices: 352 us -> 393 us
  starting transfers between devices: 125 us -> 109 us
    pallas_call x0 -> x7, Pallas kernels: none -> 324 us  [the longest x1 127 us: column_forward(): pl.pallas_call(functools.partial(forward_kernel, group, width, block, unr...]
    dot_general x14 -> x0, matrix products: 310 us -> none  [contract(): return jnp.einsum(spec, left, right, precision=fast)]
    convert_element_type x7 -> x0, local copies, waits for them, and re-layouts: 125 us -> none  [the longest x3 73.2 us: body(): as_float = tokens.reshape(field_shape).astype(jnp.float32)]
    unnamed x75 -> x28, local copies, waits for them, and re-layouts: 98.3 us -> 5.21 us
    another operation x6 -> x7, local copies, waits for them, and re-layouts: 94.8 us -> 3.39 us  [the longest x1 1.32 us: body(): gain_lanes = jnp.repeat(norm_gain, width)[None]]
    psum x3 -> x1, waiting for transfers between devices: 133 us -> 208 us  [body(): first_all, second_all = lax.psum((first_all, second_all), 'lat')]
    reshape x4, local copies, waits for them, and re-layouts: 107 us -> 39.5 us  [the longest x1 9.93 us: body(): jnp.concatenate(upstream_columns, axis=2).reshape(height, lanes)]
    psum x1 -> x0, blocking collectives: 58.8 us -> none  [body(): lax.psum((param_grads[0], param_grads[1], param_grads[2], param_grads[3],...]
  transfers between devices with their start and end apart: 7 -> 9, of which waited for: 4 -> 6; matrix products, arithmetic and copies ran while one was open for 30% -> 9% of each run, Pallas kernels for 0% -> 30%
where the time goes in v1:
time: 937 us; the launch traced here: 933 us
  waiting for transfers between devices  393 us (42%)
  Pallas kernels  324 us (35%)
  starting transfers between devices  109 us (12%)
  local copies, waits for them, and re-layouts  69.7 us (7%)
  other arithmetic  23.4 us (2%)
  between operations  14.4 us (2%)
    psum x1, waiting for transfers between devices, body(): first_all, second_all = lax.psum((first_all, second_all), 'lat')  208 us
    all_to_all x6, waiting for transfers between devices, swap(): lax.all_to_all(values, 'lat', split_axis=0, concat_axis=0, tiled=True)  183 us
    pallas_call x1, Pallas kernels, column_forward(): pl.pallas_call(functools.partial(forward_kernel, group, width, block, unr...  127 us
    all_to_all x6, starting transfers between devices, swap(): lax.all_to_all(values, 'lat', split_axis=0, concat_axis=0, tiled=True)  106 us
    pallas_call x1, Pallas kernels, column_backward(): pl.pallas_call(functools.partial(backward_kernel, group, width, block, un...  102 us
    pallas_call x5, Pallas kernels, row_call(): pl.pallas_call(kernel, grid=(samples,), in_specs=[specs[kind] for kind in...  95.1 us
  transfers between devices with their start and end apart: 9, of which 6 were waited for; matrix products, arithmetic and copies ran while one was open for 9% of the time, Pallas kernels for 30%

profile of v1, /device:TPU:0, one launch (start us, length us, event | category | flops | bytes accessed | tf_op | source)
XLA Modules:
  0.0 933.0 jit_solution(234166891538377585)
XLA Ops:
  7.2 3.7 slice.96
  10.9 7.4 all-to-all-start
  18.4 13.2 %stats.1 = (f32[16,4,180]{2,1,0:T(4,128)}, f32[16,4,180]{2,1,0:T(4,128)}) custom-call(bf16[16,4,69120]{2,1,0:T(4,128)(2,1)} %x_ref.9), custom_call_target="tpu_custom_call" | custom-call | flops 8847360000 | bytes 17694720 | tf_op jit(solution)/shard_map/stats/pallas_call | solution.py:436
  32.5 1.6 collective-permute-start
  34.1 1.3 broadcast_in_dim_reshape.6.gain_ref
  35.6 1.3 broadcast_in_dim_reshape.7.shift_ref
  36.9 1.4 collective-permute-done
  38.3 0.9 fusion.12
  40.6 17.1 %norm.1.normed_ref = bf16[16,4,69120]{2,1,0:T(4,128)(2,1)} custom-call(bf16[16,4,69120]{2,1,0:T(4,128)(2,1)} %x_ref.9, f32[16,4,180]{2,1,0:T(4,128)} %fusion.8.center_ref, f32[16,4,180]{2,1,0:T(4,128)} %fusion.7.inv_ref, f32[1,69120]{1,0:T(1,128)} %broadcast_in_dim_reshape.6.gain_ref, f32[1,69120]{1,0:T(1,128)} %broadcast_in_dim_reshape.7.shift_ref), custom_call_target="tpu_custom_call" | custom-call | flops 8847360000 | bytes 53084160 | tf_op jit(solution)/shard_map/norm/pallas_call | solution.py:436
  57.7 3.6 all-to-all-done
  61.3 1.3 copy-done
  62.6 11.7 %all-to-all-start.1 = ((bf16[16,4,69120]{2,1,0:T(4,128)(2,1)}), bf16[16,4,69120]{2,1,0:T(4,128)(2,1)}, u32[]{:S(2)}, u32[]{:S(2)}) async-start(bf16[16,4,69120]{2,1,0:T(4,128)(2,1)} %norm.1.normed_ref), calls=%async_computation.1 | async-start | bytes 17694720 | tf_op jit(solution)/shard_map/all_to_all | solution.py:455
  74.4 8.0 slice.97
  82.4 0.9 copy.45.second_bias_ref
  83.5 0.9 copy.43.first_bias_ref
  84.9 1.4 copy.42.first_ref
  86.4 146.6 %all-to-all-done.1 = bf16[16,4,69120]{2,1,0:T(4,128)(2,1)} async-done(((bf16[16,4,69120]{2,1,0:T(4,128)(2,1)}), bf16[16,4,69120]{2,1,0:T(4,128)(2,1)}, u32[]{:S(2)}, u32[]{:S(2)}) %all-to-all-start.1) | async-done | bytes 8847392 | tf_op jit(solution)/shard_map/all_to_all | solution.py:455
  232.9 38.4 %all-to-all-start.2 = ((bf16[16,4,51840]{2,1,0:T(4,128)(2,1)}), bf16[16,4,51840]{2,1,0:T(4,128)(2,1)}, u32[]{:S(2)}, u32[]{:S(2)}) async-start(bf16[16,4,51840]{2,1,0:T(4,128)(2,1)} %slice.97), calls=%async_computation.2 | async-start | bytes 13271040 | tf_op jit(solution)/shard_map/all_to_all | solution.py:455
  271.8 1.4 copy.44.second_ref
  273.2 0.9 convert_bitcast_fusion.1.first_ref
  274.1 0.9 convert_bitcast_fusion.second_ref
  275.0 9.9 %reshape.41.x_ref = bf16[64,69120]{1,0:T(8,128)(2,1)} reshape(bf16[16,4,69120]{2,1,0:T(4,128)(2,1)} %all-to-all-done.1) | data formatting | bytes 17694720 | tf_op jit(solution)/shard_map/reshape | solution.py:548
  285.0 126.7 %column_forward.1 = (bf16[64,69120]{1,0:T(8,128)(2,1)}, bf16[4,32,192,256]{3,2,1,0:T(8,128)(2,1)}, bf16[4,32,192,256]{3,2,1,0:T(8,128)(2,1)}, bf16[4,32,192,256]{3,2,1,0:T(8,128)(2,1)}, bf16[4,32,192,256]{3,2,1,0:T(8,128)(2,1)}) custom-call(bf16[64,69120]{1,0:T(8,128)(2,1)} %reshape.41.x_ref, bf16[64,128]{1,0:T(8,128)(2,1)} %constant.34.lat_ref, ...), custom_call_target="tpu_custom_call" | custom-call | flops 125829120000 | bytes 68026368 | tf_op jit(solution)/shard_map/column_forward/pallas_call | solution.py:271
  411.6 9.8 %reshape.42 = bf16[16,4,69120]{2,1,0:T(4,128)(2,1)} reshape(bf16[64,69120]{1,0:T(8,128)(2,1)} %get-tuple-element.41) | data formatting | bytes 17694720 | tf_op jit(solution)/shard_map/reshape | solution.py:551
  421.5 6.1 all-to-all-start.3
  427.6 8.1 pad_maximum_fusion
  435.8 9.9 %reshape.43.x_ref = bf16[64,69120]{1,0:T(8,128)(2,1)} reshape(bf16[16,4,69120]{2,1,0:T(4,128)(2,1)} %pad_maximum_fusion) | data formatting | bytes 17694720 | tf_op jit(solution)/shard_map/reshape | solution.py:555
  445.7 101.7 %column_backward.1 = (bf16[64,69120]{1,0:T(8,128)(2,1)}, f32[4,192,192]{2,1,0:T(8,128)}, f32[4,192,128]{2,1,0:T(8,128)}, f32[4,192,192]{2,1,0:T(8,128)}, f32[4,192,128]{2,1,0:T(8,128)}) custom-call(bf16[64,69120]{1,0:T(8,128)(2,1)} %reshape.43.x_ref, bf16[4,32,192,256]{3,2,1,0:T(8,128)(2,1)} %get-tuple-element.44.spec_ref, ...), custom_call_target="tpu_custom_call" | custom-call | flops 125829120000 | bytes 68026368 | tf_op jit(solution)/shard_map/column_backward/pallas_call | solution.py:300
  547.5 9.8 %reshape.44 = bf16[16,4,69120]{2,1,0:T(4,128)(2,1)} reshape(bf16[64,69120]{1,0:T(8,128)(2,1)} %get-tuple-element.48) | data formatting | bytes 17694720 | tf_op jit(solution)/shard_map/reshape | solution.py:559
  557.3 28.9 %all-to-all-done.3.filtered_ref = bf16[16,4,69120]{2,1,0:T(4,128)(2,1)} async-done(((bf16[16,4,69120]{2,1,0:T(4,128)(2,1)}), bf16[16,4,69120]{2,1,0:T(4,128)(2,1)}, u32[]{:S(2)}, u32[]{:S(2)}) %all-to-all-start.3) | async-done | bytes 8847392 | tf_op jit(solution)/shard_map/all_to_all | solution.py:455
  586.2 38.4 %all-to-all-start.4 = ((bf16[16,4,69120]{2,1,0:T(4,128)(2,1)}), bf16[16,4,69120]{2,1,0:T(4,128)(2,1)}, u32[]{:S(2)}, u32[]{:S(2)}) async-start(bf16[16,4,69120]{2,1,0:T(4,128)(2,1)} %reshape.44), calls=%async_computation.4 | async-start | bytes 17694720 | tf_op jit(solution)/shard_map/all_to_all | solution.py:455
  626.0 0.9 pad_maximum_fusion.4
  626.9 0.9 pad_maximum_fusion.3
  627.9 18.1 %result.1 = bf16[16,4,69120]{2,1,0:T(4,128)(2,1)} custom-call(bf16[16,4,69120]{2,1,0:T(4,128)(2,1)} %x_ref.9, bf16[16,4,69120]{2,1,0:T(4,128)(2,1)} %norm.1.normed_ref, bf16[16,4,69120]{2,1,0:T(4,128)(2,1)} %all-to-all-done.3.filtered_ref), custom_call_target="tpu_custom_call" | custom-call | flops 8847360000 | bytes 35389440 | tf_op jit(solution)/shard_map/result/pallas_call | solution.py:436
  646.0 208.3 %all-reduce.3.cloned.1.call-done = (f32[2,4,97,96]{2,3,1,0:T(8,128)}, f32[2,4,97,96]{2,3,1,0:T(8,128)}) async-done(((f32[2,4,97,96]{2,3,1,0:T(8,128)}, f32[2,4,97,96]{2,3,1,0:T(8,128)}), (f32[2,4,97,96]{2,3,1,0:T(8,128)}, f32[2,4,97,96]{2,3,1,0:T(8,128)})) %all-reduce.3.cloned.1.call-update) | async-done | bytes 595984 | tf_op jit(solution)/shard_map/psum | solution.py:571
  854.3 1.9 slice_reduce_fusion.1
  856.2 1.9 copy.50
  858.2 1.9 copy.49
  860.1 23.1 %sums.1 = (f32[16,4,180]{2,1,0:T(4,128)}, f32[16,4,180]{2,1,0:T(4,128)}, f32[4,69120]{1,0:T(4,128)}, f32[4,69120]{1,0:T(4,128)}) custom-call(bf16[16,4,69120]{2,1,0:T(4,128)(2,1)} %x_ref.9, bf16[16,4,69120]{2,1,0:T(4,128)(2,1)} %up_ref.3, bf16[16,4,69120]{2,1,0:T(4,128)(2,1)} %all-to-all-done.4.grad_ref, f32[16,4,180]{2,1,0:T(4,128)} %fusion.8.center_ref, ...), custom_call_target="tpu_custom_call" | custom-call | flops 8847360000 | bytes 61931520 | tf_op jit(solution)/shard_map/sums/pallas_call | solution.py:436
  883.2 0.9 pad_maximum_fusion.6
  884.1 1.5 collective-permute-start.1
  885.6 1.9 reduce_sum.61
  888.2 1.9 reduce_sum.64
  891.5 3.7 all-to-all-start.5
  895.2 1.0 slice_reduce_fusion
  896.2 0.9 fusion.11
  897.8 4.2 all-to-all-done.5
  902.6 23.6 %final.1 = bf16[16,4,69120]{2,1,0:T(4,128)(2,1)} custom-call(bf16[16,4,69120]{2,1,0:T(4,128)(2,1)} %x_ref.9, bf16[16,4,69120]{2,1,0:T(4,128)(2,1)} %up_ref.3, bf16[16,4,69120]{2,1,0:T(4,128)(2,1)} %all-to-all-done.4.grad_ref, f32[16,4,180]{2,1,0:T(4,128)} %fusion.8.center_ref, f32[16,4,180]{2,1,0:T(4,128)} %fusion.7.inv_ref, ...), custom_call_target="tpu_custom_call" | custom-call | flops 8847360000 | bytes 79626240 | tf_op jit(solution)/shard_map/final/pallas_call | solution.py:436
  (69 shorter events, 8.3 us)
Async XLA Ops:
  10.9 50.4 %all-to-all-start = ((bf16[16,4,17280]{2,1,0:T(4,128)(2,1)}), bf16[16,4,17280]{2,1,0:T(4,128)(2,1)S(1)}, u32[]{:S(2)}, u32[]{:S(2)}) async-start(bf16[16,4,17280]{2,1,0:T(4,128)(2,1)} %slice.96), calls=%async_computation | async-start | bytes 4423680 | tf_op jit(solution)/shard_map/all_to_all | solution.py:455
  18.3 15.7 %copy-start.11 = (f32[384]{0:T(512)S(1)}, f32[384]{0:T(512)}, u32[]{:S(2)}) copy-start(f32[384]{0:T(512)} %param.15) | copy-start | bytes 4612
  18.3 17.1 %copy-start.12 = (f32[384]{0:T(512)S(1)}, f32[384]{0:T(512)}, u32[]{:S(2)}) copy-start(f32[384]{0:T(512)} %param.16) | copy-start | bytes 4612
  32.5 5.9 collective-permute-start
  61.3 1.3 copy-start
  62.6 170.3 %all-to-all-start.1 = ((bf16[16,4,69120]{2,1,0:T(4,128)(2,1)}), bf16[16,4,69120]{2,1,0:T(4,128)(2,1)}, u32[]{:S(2)}, u32[]{:S(2)}) async-start(bf16[16,4,69120]{2,1,0:T(4,128)(2,1)} %norm.1.normed_ref), calls=%async_computation.1 | async-start | bytes 17694720 | tf_op jit(solution)/shard_map/all_to_all | solution.py:455
  74.4 8.0 copy-start.9
  74.4 9.0 copy-start.10
  74.4 10.0 %copy-start.3 = (f32[2,4,96,96]{3,2,1,0:T(8,128)S(1)}, f32[2,4,96,96]{3,2,1,0:T(8,128)}, u32[]{:S(2)}) copy-start(f32[2,4,96,96]{3,2,1,0:T(8,128)} %param.17) | copy-start | bytes 884740
  82.4 4.0 copy-start.4
  232.9 188.5 %all-to-all-start.2 = ((bf16[16,4,51840]{2,1,0:T(4,128)(2,1)}), bf16[16,4,51840]{2,1,0:T(4,128)(2,1)}, u32[]{:S(2)}, u32[]{:S(2)}) async-start(bf16[16,4,51840]{2,1,0:T(4,128)(2,1)} %slice.97), calls=%async_computation.2 | async-start | bytes 13271040 | tf_op jit(solution)/shard_map/all_to_all | solution.py:455
  421.5 6.2 copy-start.1
  421.5 164.7 %all-to-all-start.3 = ((bf16[16,4,69120]{2,1,0:T(4,128)(2,1)}), bf16[16,4,69120]{2,1,0:T(4,128)(2,1)}, u32[]{:S(2)}, u32[]{:S(2)}) async-start(bf16[16,4,69120]{2,1,0:T(4,128)(2,1)} %reshape.42), calls=%async_computation.3 | async-start | bytes 17694720 | tf_op jit(solution)/shard_map/all_to_all | solution.py:455
  557.3 67.3 %copy-start.8 = (f32[4,192,128]{2,1,0:T(8,128)S(1)}, f32[4,192,128]{2,1,0:T(8,128)}, u32[]{:S(2)}) copy-start(f32[4,192,128]{2,1,0:T(8,128)} %get-tuple-element.53) | copy-start | bytes 1179652
  557.3 67.6 %copy-start.7 = (f32[4,192,128]{2,1,0:T(8,128)S(1)}, f32[4,192,128]{2,1,0:T(8,128)}, u32[]{:S(2)}) copy-start(f32[4,192,128]{2,1,0:T(8,128)} %get-tuple-element.55) | copy-start | bytes 1179652
  557.3 68.4 %copy-start.5 = (f32[4,192,192]{2,1,0:T(8,128)S(1)}, f32[4,192,192]{2,1,0:T(8,128)}, u32[]{:S(2)}) copy-start(f32[4,192,192]{2,1,0:T(8,128)} %get-tuple-element.52) | copy-start | bytes 1769476
  557.3 68.4 %copy-start.6 = (f32[4,192,192]{2,1,0:T(8,128)S(1)}, f32[4,192,192]{2,1,0:T(8,128)}, u32[]{:S(2)}) copy-start(f32[4,192,192]{2,1,0:T(8,128)} %get-tuple-element.54) | copy-start | bytes 1769476
  586.2 268.1 %all-to-all-start.4 = ((bf16[16,4,69120]{2,1,0:T(4,128)(2,1)}), bf16[16,4,69120]{2,1,0:T(4,128)(2,1)}, u32[]{:S(2)}, u32[]{:S(2)}) async-start(bf16[16,4,69120]{2,1,0:T(4,128)(2,1)} %reshape.44), calls=%async_computation.4 | async-start | bytes 17694720 | tf_op jit(solution)/shard_map/all_to_all | solution.py:455
  624.6 229.7 %all-reduce.3.cloned.1.call-start = ((), (), s32[]{:S(2)}) async-start(), calls=%async_computation.6 | async-start | bytes 1572864 | tf_op jit(solution)/shard_map/psum | solution.py:571
  860.1 35.1 %copy-start.2 = (f32[2,4,97,96]{2,3,1,0:T(8,128)S(1)}, f32[2,4,97,96]{2,3,1,0:T(8,128)}, u32[]{:S(2)}) copy-start(f32[2,4,97,96]{2,3,1,0:T(8,128)} %get-tuple-element.61) | copy-start | bytes 893956
  884.1 12.1 %collective-permute-start.1 = (f32[2,16,4,180]{3,2,1,0:T(4,128)S(1)}, f32[2,16,4,180]{3,2,1,0:T(4,128)S(1)}, u32[]{:S(2)}, u32[]{:S(2)}) collective-permute-start(f32[2,16,4,180]{3,2,1,0:T(4,128)S(1)} %pad_maximum_fusion.6), channel_id=1, source_target_pairs={{0,1},{1,0},{2,3},{3,2},{4,5},{5,4},{6,7},{7,6},{8,9},{9,8},{10,11... | collective-permute-start | bytes 276488 | tf_op jit(solution)/shard_map/ppermute | solution.py:461
  891.5 10.5 %all-to-all-start.5 = ((f32[16,2,384]{2,1,0:T(2,128)}), f32[16,2,384]{2,1,0:T(2,128)S(1)}, u32[]{:S(2)}, u32[]{:S(2)}) async-start(f32[16,2,384]{2,1,0:T(2,128)} %broadcast_in_dim.30), calls=%async_computation.5 | async-start | bytes 98304 | tf_op jit(solution)/shard_map/all_to_all | solution.py:455
Sparse Core Ops, SparseCore 0:
  629.4 224.8 all-reduce.2
